TPU v7x, 32 devices: a whole 2x2x4 slice. The times are simulated.
32 devices in a mesh: seq: 8 (over z, x), kvh: 4 (over y, core).
Axes of the slice: x: 2, y: 2, z: 4, core: 2. Of those that a mesh axis runs over, the one named last changes fastest.
Arguments:
- queries: bfloat16 [1024, 28, 128], P('seq', 'kvh'), may hold values from -80 to 80
- new_keys: bfloat16 [1024, 4, 128], P('seq', 'kvh'), may hold values from -8 to 8
- cache_keys: bfloat16 [512, 4, 128], P('seq', 'kvh'), may hold values from -1.1953125 to 1.1953125
- window_start: int32 [8], replicated, may hold values from 0 to 512, as said below
- owner_slot: int32 [8], replicated, may hold values from 0 to 511, as said below
Outputs:
- relevance: bfloat16 [1024, 28, 512], P('seq', 'kvh')
- rep_bank: bfloat16 [512, 4, 128], P('seq', 'kvh')
Inputs may be any that keep to these rules, and one draw needn't show every extreme that they name: `window_start`: each window lies inside the new tokens; some window begins at the first new token and some ends at the last. `owner_slot`: the slots are distinct; the first and the last memory block are always among them.
All inputs are finite; a program needn't handle non-finite values.
Results may differ from a plain program's by a relative error of at most 0.0018.
Values may be sent and summed in bfloat16 or wider, within the bound.
A program may use at most 64 MiB of HBM per device.

v0:
```python
import math
import jax
import jax.numpy as jnp
from jax import lax
from jax.sharding import PartitionSpec as P

BLK = 128
WIN = 512


def row_scores(query_rows, key_rows):
    return lax.dot_general(
        query_rows, key_rows, (((1,), (1,)), ((), ())), preferred_element_type=jnp.float32
    )


def per_device(queries, new_keys, cache_keys, window_start, owner_slot):
    tok_count, group_size, head_dim = queries.shape
    score_scale = 1.0 / math.sqrt(head_dim)
    query_rows = queries.reshape(tok_count * group_size, head_dim)
    device_index = lax.axis_index("seq")
    keys_all = lax.all_gather(new_keys, "seq", axis=0, tiled=True)
    key_flat = keys_all[:, 0, :]
    total_tokens = key_flat.shape[0]
    block_count = total_tokens // BLK
    group_blocks = math.gcd(block_count, 8)
    position = device_index * tok_count + jnp.arange(tok_count, dtype=jnp.int32)
    row_position = jnp.repeat(position, group_size)
    inside = (row_position[:, None] >= window_start[None, :]) & (
        row_position[:, None] < window_start[None, :] + WIN
    )
    inside = inside.astype(jnp.float32)
    key_groups = key_flat.reshape(block_count // group_blocks, group_blocks * BLK, head_dim)
    inside_groups = inside.reshape(
        query_rows.shape[0], block_count // group_blocks, group_blocks
    ).transpose(1, 0, 2)

    def group_sums(members):
        key_part, mask_part = members
        scores = row_scores(query_rows, key_part) * score_scale
        scores = scores.reshape(query_rows.shape[0], group_blocks, BLK)
        softmax_weights = jax.nn.softmax(scores, axis=-1)
        return jnp.einsum("rgk,rg->gk", softmax_weights, mask_part)

    colsum = lax.map(group_sums, (key_groups, inside_groups)).reshape(block_count, BLK)
    colsum = lax.psum(colsum, "seq")
    weights = colsum / (group_size * WIN)
    representative = jnp.einsum(
        "nr,nrz->nz",
        weights,
        key_flat.reshape(block_count, BLK, head_dim).astype(jnp.float32),
        precision=lax.Precision.HIGHEST,
    ).astype(jnp.bfloat16)
    rep_float = representative.astype(jnp.float32)
    local_blocks = cache_keys.shape[0]
    slot_ids = device_index * local_blocks + jnp.arange(local_blocks, dtype=jnp.int32)
    matches = (owner_slot[:, None] == slot_ids[None, :]).astype(jnp.float32)
    placed = jnp.dot(matches.T, rep_float, precision=lax.Precision.HIGHEST)
    slot_taken = jnp.sum(matches, axis=0) > 0.5
    new_shard = jnp.where(slot_taken[:, None], placed.astype(jnp.bfloat16), cache_keys[:, 0, :])
    totals = (
        row_scores(query_rows, lax.all_gather(new_shard, "seq", axis=0, tiled=True)) * score_scale
    )
    relevance = totals.astype(jnp.bfloat16).reshape(tok_count, group_size, totals.shape[1])
    return (relevance, new_shard[:, None, :])


def solution(mesh):
    return jax.shard_map(
        per_device,
        mesh=mesh,
        in_specs=(P("seq", "kvh", None), P("seq", "kvh", None), P("seq", "kvh", None), P(), P()),
        out_specs=(P("seq", "kvh", None), P("seq", "kvh", None)),
        check_vma=False,
    )
```

profile of v0, /device:TPU:0, one launch (start us, length us, event | category | flops | bytes accessed | tf_op | source)
XLA Modules:
  0.0 238.6 jit_solution(1154057495097289812)
XLA Ops:
  0.6 1.1 copy.14
  1.7 0.1 reshape.33
  1.8 32.8 %all_gather.6 = bf16[1024,1,128]{2,0,1:T(8,128)(2,1)S(1)} all-gather(bf16[128,1,128]{2,0,1:T(8,128)(2,1)} %param.6), channel_id=1, replica_groups=mesh['seq'=8,'kvh'=4] {'seq'}, dimensions={0}, use_global_device_ids=true | all-gather | bytes 294912 | tf_op jit(solution)/shard_map/all_gather | solution.py:22
  34.6 0.6 multiply_bitcast_fusion
  35.2 0.9 copy.22
  36.1 145.2 %fusion.12 = (f32[896,8]{1,0:T(8,128)S(1)}, f32[896,8,128]{2,1,0:T(8,128)S(1)}) fusion(f32[896,8,128]{2,1,0:T(8,128)S(1)} %bitcast.27), kind=kOutput, calls=%fused_computation.24 | output fusion | flops 1835135 | bytes 7368704 | tf_op jit(solution)/shard_map/while/body/eval_jaxpr/sub | solution.py:42
  181.3 0.0 copy-start.1
  181.3 0.0 copy-start.3
  181.3 0.0 copy-start.2
  181.4 1.2 broadcast_divide_fusion
  182.6 0.1 broadcast_in_dim.28
  182.7 0.2 ge.15
  182.9 0.0 copy-done.1
  182.9 0.1 and_bitcast_fusion
  183.0 0.5 fusion.1
  183.5 21.4 %psum.7 = f32[8,128]{1,0:T(8,128)S(1)} all-reduce(f32[8,128]{1,0:T(8,128)S(1)} %bitcast.32), channel_id=1, replica_groups=mesh['seq'=8,'kvh'=4] {'seq'}, use_global_device_ids=true, to_apply=%region_3.4 | all-reduce | flops 1024 | bytes 8192 | tf_op jit(solution)/shard_map/psum | solution.py:46
  204.9 0.3 fusion.13
  205.2 0.0 copy-done.3
  205.2 0.1 fusion.8
  205.3 0.0 copy-done.2
  205.3 0.3 fusion.4
  205.6 0.0 copy-start
  205.6 30.5 %all_gather.7 = bf16[512,128]{1,0:T(8,128)(2,1)S(1)} all-gather(bf16[64,128]{1,0:T(8,128)(2,1)S(1)} %fusion.4), channel_id=1, replica_groups=mesh['seq'=8,'kvh'=4] {'seq'}, dimensions={0}, use_global_device_ids=true | all-gather | bytes 147456 | tf_op jit(solution)/shard_map/all_gather | solution.py:62
  236.1 0.4 fusion.3
  236.5 0.5 copy.15
  237.0 0.3 reshape.35
  237.3 1.2 copy.16
  238.6 0.0 copy-done
  (5 shorter events, 0.0 us)
Async XLA Ops:
  181.3 1.6 copy-start.1
  181.3 23.9 %copy-start.3 = (s32[8]{0:T(128)S(1)}, s32[8]{0:T(128)}, u32[]{:S(2)}) copy-start(s32[8]{0:T(128)} %param.9) | copy-start | bytes 100
  181.3 24.0 %copy-start.2 = (bf16[64,1,128]{2,0,1:T(8,128)(2,1)S(1)}, bf16[64,1,128]{2,0,1:T(8,128)(2,1)}, u32[]{:S(2)}) copy-start(bf16[64,1,128]{2,0,1:T(8,128)(2,1)} %param.7) | copy-start | bytes 49156
  205.6 33.0 %copy-start = (bf16[64,128]{1,0:T(8,128)(2,1)}, bf16[64,128]{1,0:T(8,128)(2,1)S(1)}, u32[]{:S(2)}) copy-start(bf16[64,128]{1,0:T(8,128)(2,1)S(1)} %fusion.4) | copy-start | bytes 49156
where the time goes:
time: 239 us
  other arithmetic  147 us (62%)
  blocking collectives  84.7 us (35%)
  local copies, waits for them, and re-layouts  4.46 us (2%)
    sub x1, other arithmetic, group_sums(): softmax_weights = jax.nn.softmax(scores, axis=-1)  145 us
    all_gather x1, blocking collectives, per_device(): keys_all = lax.all_gather(new_keys, 'seq', axis=0, tiled=True)  32.8 us
    all_gather x1, blocking collectives, per_device(): lax.all_gather(new_shard, 'seq', axis=0, tiled=True)  30.5 us
    psum x1, blocking collectives, per_device(): colsum = lax.psum(colsum, 'seq')  21.4 us

commit v1 on v0

--- a/solution.py
+++ b/solution.py
@@ -1,11 +1,32 @@
+import functools
 import math
 import jax
 import jax.numpy as jnp
 from jax import lax
 from jax.sharding import PartitionSpec as P
+from jax.lax import axis_index, axis_size, ppermute
 
 BLK = 128
 WIN = 512
+
+
+def start_skins(q_in, mesh_name):
+    fan = axis_size(mesh_name)
+    u_next = sorted(((nth, (nth + 1) % fan) for nth in range(fan)))
+    r2 = q_in
+    line_up = [r2]
+    ix = 1
+    while ix < fan:
+        r2 = ppermute(r2, mesh_name, u_next)
+        line_up.insert(0, r2)
+        ix = ix + 1
+    x_now = jnp.concatenate(line_up, axis=0)
+    seen_now = axis_index(mesh_name)
+    newest = seen_now + 1
+    return jnp.roll(x_now, newest * q_in.shape[0], axis=0)
+
+
+_load_figure = functools.partial(start_skins, mesh_name="seq")
 
 
 def row_scores(query_rows, key_rows):
@@ -19,7 +40,7 @@
     score_scale = 1.0 / math.sqrt(head_dim)
     query_rows = queries.reshape(tok_count * group_size, head_dim)
     device_index = lax.axis_index("seq")
-    keys_all = lax.all_gather(new_keys, "seq", axis=0, tiled=True)
+    keys_all = _load_figure(new_keys)
     key_flat = keys_all[:, 0, :]
     total_tokens = key_flat.shape[0]
     block_count = total_tokens // BLK

time: 239 us -> 104 us (0.44)
  other arithmetic: 147 us -> 2.8 us
  waiting for transfers between devices: 0 us -> 41.5 us
  blocking collectives: 84.7 us -> 47.6 us
  starting transfers between devices: 0 us -> 3.04 us
    sub x1 -> x0, other arithmetic: 145 us -> none  [group_sums(): softmax_weights = jax.nn.softmax(scores, axis=-1)]
    ppermute x0 -> x7, waiting for transfers between devices: none -> 41.5 us  [start_skins(): r2 = ppermute(r2, mesh_name, u_next)]
    all_gather x1 -> x0, blocking collectives: 32.8 us -> none  [per_device(): keys_all = lax.all_gather(new_keys, 'seq', axis=0, tiled=True)]
    psum x1, blocking collectives: 21.4 us -> 17.1 us  [per_device(): colsum = lax.psum(colsum, 'seq')]
    ppermute x0 -> x7, starting transfers between devices: none -> 3.04 us  [start_skins(): r2 = ppermute(r2, mesh_name, u_next)]
  transfers between devices with their start and end apart: 0 -> 7, of which waited for: 0 -> 7; matrix products, arithmetic and copies ran while one was open for 0% -> 3% of each run, Pallas kernels for 0% -> 0%
where the time goes in v1:
time: 104 us
  blocking collectives  47.6 us (46%)
  waiting for transfers between devices  41.5 us (40%)
  local copies, waits for them, and re-layouts  5.48 us (5%)
  starting transfers between devices  3.04 us (3%)
  other arithmetic  2.8 us (3%)
  matrix products  2.45 us (2%)
    ppermute x7, waiting for transfers between devices, start_skins(): r2 = ppermute(r2, mesh_name, u_next)  41.5 us
    all_gather x1, blocking collectives, per_device(): lax.all_gather(new_shard, 'seq', axis=0, tiled=True)  30.5 us
    psum x1, blocking collectives, per_device(): colsum = lax.psum(colsum, 'seq')  17.1 us
    unnamed x23, local copies, waits for them, and re-layouts  3.25 us
    ppermute x7, starting transfers between devices, start_skins(): r2 = ppermute(r2, mesh_name, u_next)  3.04 us
  transfers between devices with their start and end apart: 7, of which 7 were waited for; matrix products, arithmetic and copies ran while one was open for 3% of the time, Pallas kernels for 0%

profile of v1, /device:TPU:0, one launch (start us, length us, event | category | flops | bytes accessed | tf_op | source)
XLA Modules:
  0.0 103.7 jit_solution(3255974162189516865)
XLA Ops:
  0.6 3.0 %collective-permute-start = (bf16[128,1,128]{2,0,1:T(8,128)(2,1)}, bf16[128,1,128]{2,0,1:T(8,128)(2,1)S(1)}, u32[]{:S(2)}, u32[]{:S(2)}) collective-permute-start(bf16[128,1,128]{2,0,1:T(8,128)(2,1)} %param.6), channel_id=1, source_target_pairs={{0,4},{4,8},{8,12},{12,16},{16,20},{20,24},{24,28},{28,0},{1,5},{5... | collective-permute-start | bytes 98312 | tf_op jit(solution)/shard_map/ppermute | solution.py:20
  3.6 5.1 %collective-permute-done = bf16[128,1,128]{2,0,1:T(8,128)(2,1)S(1)} collective-permute-done((bf16[128,1,128]{2,0,1:T(8,128)(2,1)}, bf16[128,1,128]{2,0,1:T(8,128)(2,1)S(1)}, u32[]{:S(2)}, u32[]{:S(2)}) %collective-permute-start) | collective-permute-done | bytes 32800 | tf_op jit(solution)/shard_map/ppermute | solution.py:20
  8.8 0.0 collective-permute-start.1
  8.8 0.7 broadcast_add_fusion
  9.5 6.0 %collective-permute-done.1 = bf16[128,1,128]{2,0,1:T(8,128)(2,1)S(1)} collective-permute-done((bf16[128,1,128]{2,0,1:T(8,128)(2,1)S(1)}, bf16[128,1,128]{2,0,1:T(8,128)(2,1)S(1)}, u32[]{:S(2)}, u32[]{:S(2)}) %collective-permute-start.1) | collective-permute-done | bytes 32800 | tf_op jit(solution)/shard_map/ppermute | solution.py:20
  15.4 0.0 collective-permute-start.2
  15.4 0.1 broadcast_in_dim.28
  15.5 0.2 ge.15
  15.7 6.3 %collective-permute-done.2 = bf16[128,1,128]{2,0,1:T(8,128)(2,1)S(1)} collective-permute-done((bf16[128,1,128]{2,0,1:T(8,128)(2,1)S(1)}, bf16[128,1,128]{2,0,1:T(8,128)(2,1)S(1)}, u32[]{:S(2)}, u32[]{:S(2)}) %collective-permute-start.2) | collective-permute-done | bytes 32800 | tf_op jit(solution)/shard_map/ppermute | solution.py:20
  22.0 0.0 collective-permute-start.3
  22.0 0.7 and_bitcast_fusion
  22.8 5.9 %collective-permute-done.3 = bf16[128,1,128]{2,0,1:T(8,128)(2,1)S(1)} collective-permute-done((bf16[128,1,128]{2,0,1:T(8,128)(2,1)S(1)}, bf16[128,1,128]{2,0,1:T(8,128)(2,1)S(1)}, u32[]{:S(2)}, u32[]{:S(2)}) %collective-permute-start.3) | collective-permute-done | bytes 32800 | tf_op jit(solution)/shard_map/ppermute | solution.py:20
  28.6 0.0 collective-permute-start.4
  28.6 6.9 %collective-permute-done.4 = bf16[128,1,128]{2,0,1:T(8,128)(2,1)S(1)} collective-permute-done((bf16[128,1,128]{2,0,1:T(8,128)(2,1)S(1)}, bf16[128,1,128]{2,0,1:T(8,128)(2,1)S(1)}, u32[]{:S(2)}, u32[]{:S(2)}) %collective-permute-start.4) | collective-permute-done | bytes 32800 | tf_op jit(solution)/shard_map/ppermute | solution.py:20
  35.6 0.0 collective-permute-start.5
  35.6 0.7 fusion.13
  36.3 5.9 %collective-permute-done.5 = bf16[128,1,128]{2,0,1:T(8,128)(2,1)S(1)} collective-permute-done((bf16[128,1,128]{2,0,1:T(8,128)(2,1)S(1)}, bf16[128,1,128]{2,0,1:T(8,128)(2,1)S(1)}, u32[]{:S(2)}, u32[]{:S(2)}) %collective-permute-start.5) | collective-permute-done | bytes 32800 | tf_op jit(solution)/shard_map/ppermute | solution.py:20
  42.2 0.0 collective-permute-start.6
  42.2 1.1 %copy.14 = bf16[128,7,128]{2,1,0:T(8,128)(2,1)S(1)} copy(bf16[128,7,128]{2,0,1:T(8,128)(2,1)} %param.5) | data formatting | bytes 458752 | tf_op args[0]
  43.3 0.1 reshape.33
  43.4 5.4 %collective-permute-done.6 = bf16[128,1,128]{2,0,1:T(8,128)(2,1)S(1)} collective-permute-done((bf16[128,1,128]{2,0,1:T(8,128)(2,1)S(1)}, bf16[128,1,128]{2,0,1:T(8,128)(2,1)S(1)}, u32[]{:S(2)}, u32[]{:S(2)}) %collective-permute-start.6) | collective-permute-done | bytes 32800 | tf_op jit(solution)/shard_map/ppermute | solution.py:20
  48.9 0.8 constant_dynamic-update-slice_fusion.8
  49.8 0.8 constant_dynamic-update-slice_fusion
  50.6 0.6 bitcast_reduce_fusion
  51.2 0.7 fusion.4
  51.9 0.2 broadcast.29
  52.1 0.0 copy-start.1
  52.1 0.0 copy-start.2
  52.1 0.8 fusion.1
  53.0 17.1 %psum.7 = f32[8,128]{1,0:T(8,128)S(1)} all-reduce(f32[8,128]{1,0:T(8,128)S(1)} %bitcast.41), channel_id=1, replica_groups=mesh['seq'=8,'kvh'=4] {'seq'}, use_global_device_ids=true, to_apply=%region_3.4 | all-reduce | flops 1024 | bytes 8192 | tf_op jit(solution)/shard_map/psum | solution.py:67
  70.1 0.3 fusion.17
  70.4 0.0 copy-done.1
  70.4 0.0 copy-done.2
  70.4 0.3 fusion.8
  70.7 0.0 copy-start
  70.7 30.5 %all_gather.3 = bf16[512,128]{1,0:T(8,128)(2,1)S(1)} all-gather(bf16[64,128]{1,0:T(8,128)(2,1)S(1)} %fusion.8), channel_id=1, replica_groups=mesh['seq'=8,'kvh'=4] {'seq'}, dimensions={0}, use_global_device_ids=true | all-gather | bytes 147456 | tf_op jit(solution)/shard_map/all_gather | solution.py:83
  101.2 0.4 fusion.7
  101.6 0.5 copy.15
  102.2 0.3 reshape.35
  102.5 1.2 %copy.16 = bf16[128,7,512]{2,0,1:T(8,128)(2,1)} copy(bf16[128,7,512]{2,1,0:T(8,128)(2,1)S(1)} %reshape.35) | data formatting | bytes 1835008
  103.7 0.0 copy-done
  (19 shorter events, 0.2 us)
Async XLA Ops:
  0.6 8.2 %collective-permute-start = (bf16[128,1,128]{2,0,1:T(8,128)(2,1)}, bf16[128,1,128]{2,0,1:T(8,128)(2,1)S(1)}, u32[]{:S(2)}, u32[]{:S(2)}) collective-permute-start(bf16[128,1,128]{2,0,1:T(8,128)(2,1)} %param.6), channel_id=1, source_target_pairs={{0,4},{4,8},{8,12},{12,16},{16,20},{20,24},{24,28},{28,0},{1,5},{5... | collective-permute-start | bytes 98312 | tf_op jit(solution)/shard_map/ppermute | solution.py:20
  8.8 6.6 %collective-permute-start.1 = (bf16[128,1,128]{2,0,1:T(8,128)(2,1)S(1)}, bf16[128,1,128]{2,0,1:T(8,128)(2,1)S(1)}, u32[]{:S(2)}, u32[]{:S(2)}) collective-permute-start(bf16[128,1,128]{2,0,1:T(8,128)(2,1)S(1)} %collective-permute-done), channel_id=1, source_target_pairs={{0,4},{4,8},{8,12},{12,16},{16,20},{20,24},{24,28},{28,0},{1,5},{5... | collective-permute-start | bytes 98312 | tf_op jit(solution)/shard_map/ppermute | solution.py:20
  15.4 6.6 %collective-permute-start.2 = (bf16[128,1,128]{2,0,1:T(8,128)(2,1)S(1)}, bf16[128,1,128]{2,0,1:T(8,128)(2,1)S(1)}, u32[]{:S(2)}, u32[]{:S(2)}) collective-permute-start(bf16[128,1,128]{2,0,1:T(8,128)(2,1)S(1)} %collective-permute-done.1), channel_id=1, source_target_pairs={{0,4},{4,8},{8,12},{12,16},{16,20},{20,24},{24,28},{28,0},{1,5},{5... | collective-permute-start | bytes 98312 | tf_op jit(solution)/shard_map/ppermute | solution.py:20
  22.0 6.6 %collective-permute-start.3 = (bf16[128,1,128]{2,0,1:T(8,128)(2,1)S(1)}, bf16[128,1,128]{2,0,1:T(8,128)(2,1)S(1)}, u32[]{:S(2)}, u32[]{:S(2)}) collective-permute-start(bf16[128,1,128]{2,0,1:T(8,128)(2,1)S(1)} %collective-permute-done.2), channel_id=1, source_target_pairs={{0,4},{4,8},{8,12},{12,16},{16,20},{20,24},{24,28},{28,0},{1,5},{5... | collective-permute-start | bytes 98312 | tf_op jit(solution)/shard_map/ppermute | solution.py:20
  28.6 7.0 %collective-permute-start.4 = (bf16[128,1,128]{2,0,1:T(8,128)(2,1)S(1)}, bf16[128,1,128]{2,0,1:T(8,128)(2,1)S(1)}, u32[]{:S(2)}, u32[]{:S(2)}) collective-permute-start(bf16[128,1,128]{2,0,1:T(8,128)(2,1)S(1)} %collective-permute-done.3), channel_id=1, source_target_pairs={{0,4},{4,8},{8,12},{12,16},{16,20},{20,24},{24,28},{28,0},{1,5},{5... | collective-permute-start | bytes 98312 | tf_op jit(solution)/shard_map/ppermute | solution.py:20
  35.6 6.6 %collective-permute-start.5 = (bf16[128,1,128]{2,0,1:T(8,128)(2,1)S(1)}, bf16[128,1,128]{2,0,1:T(8,128)(2,1)S(1)}, u32[]{:S(2)}, u32[]{:S(2)}) collective-permute-start(bf16[128,1,128]{2,0,1:T(8,128)(2,1)S(1)} %collective-permute-done.4), channel_id=1, source_target_pairs={{0,4},{4,8},{8,12},{12,16},{16,20},{20,24},{24,28},{28,0},{1,5},{5... | collective-permute-start | bytes 98312 | tf_op jit(solution)/shard_map/ppermute | solution.py:20
  42.2 6.6 %collective-permute-start.6 = (bf16[128,1,128]{2,0,1:T(8,128)(2,1)S(1)}, bf16[128,1,128]{2,0,1:T(8,128)(2,1)S(1)}, u32[]{:S(2)}, u32[]{:S(2)}) collective-permute-start(bf16[128,1,128]{2,0,1:T(8,128)(2,1)S(1)} %collective-permute-done.5), channel_id=1, source_target_pairs={{0,4},{4,8},{8,12},{12,16},{16,20},{20,24},{24,28},{28,0},{1,5},{5... | collective-permute-start | bytes 98312 | tf_op jit(solution)/shard_map/ppermute | solution.py:20
  52.1 18.3 %copy-start.1 = (bf16[64,1,128]{2,0,1:T(8,128)(2,1)S(1)}, bf16[64,1,128]{2,0,1:T(8,128)(2,1)}, u32[]{:S(2)}) copy-start(bf16[64,1,128]{2,0,1:T(8,128)(2,1)} %param.7) | copy-start | bytes 49156
  52.1 18.3 %copy-start.2 = (s32[8]{0:T(128)S(1)}, s32[8]{0:T(128)}, u32[]{:S(2)}) copy-start(s32[8]{0:T(128)} %param.9) | copy-start | bytes 100
  70.7 33.0 %copy-start = (bf16[64,128]{1,0:T(8,128)(2,1)}, bf16[64,128]{1,0:T(8,128)(2,1)S(1)}, u32[]{:S(2)}) copy-start(bf16[64,128]{1,0:T(8,128)(2,1)S(1)} %fusion.8) | copy-start | bytes 49156

commit v2 on v0

--- a/solution.py
+++ b/solution.py
@@ -43,7 +43,8 @@
         return jnp.einsum("rgk,rg->gk", softmax_weights, mask_part)
 
     colsum = lax.map(group_sums, (key_groups, inside_groups)).reshape(block_count, BLK)
-    colsum = lax.psum(colsum, "seq")
+    inter = lax.all_gather(colsum, "seq")
+    colsum = jnp.sum(inter, 0)
     weights = colsum / (group_size * WIN)
     representative = jnp.einsum(
         "nr,nrz->nz",

time: 239 us -> 248 us (1.038)
  blocking collectives: 84.7 us -> 93.9 us
    all_gather x0 -> x1, blocking collectives: none -> 30.6 us  [per_device(): inter = lax.all_gather(colsum, 'seq')]
    psum x1 -> x0, blocking collectives: 21.4 us -> none  [per_device(): colsum = lax.psum(colsum, 'seq')]
where the time goes in v2:
time: 248 us
  other arithmetic  147 us (59%)
  blocking collectives  93.9 us (38%)
  local copies, waits for them, and re-layouts  4.46 us (2%)
    sub x1, other arithmetic, group_sums(): softmax_weights = jax.nn.softmax(scores, axis=-1)  145 us
    all_gather x1, blocking collectives, per_device(): keys_all = lax.all_gather(new_keys, 'seq', axis=0, tiled=True)  32.8 us
    all_gather x1, blocking collectives, per_device(): inter = lax.all_gather(colsum, 'seq')  30.6 us
    all_gather x1, blocking collectives, per_device(): lax.all_gather(new_shard, 'seq', axis=0, tiled=True)  30.5 us

profile of v2, /device:TPU:0, one launch (start us, length us, event | category | flops | bytes accessed | tf_op | source)
XLA Modules:
  0.0 247.8 jit_solution(2771014542267106605)
XLA Ops:
  0.6 1.1 copy.14
  1.7 0.1 reshape.31
  1.8 32.8 %all_gather.9 = bf16[1024,1,128]{2,0,1:T(8,128)(2,1)S(1)} all-gather(bf16[128,1,128]{2,0,1:T(8,128)(2,1)} %param.6), channel_id=1, replica_groups=mesh['seq'=8,'kvh'=4] {'seq'}, dimensions={0}, use_global_device_ids=true | all-gather | bytes 294912 | tf_op jit(solution)/shard_map/all_gather | solution.py:22
  34.6 0.6 multiply_bitcast_fusion
  35.2 0.9 copy.22
  36.1 145.2 %fusion.12 = (f32[896,8]{1,0:T(8,128)S(1)}, f32[896,8,128]{2,1,0:T(8,128)S(1)}) fusion(f32[896,8,128]{2,1,0:T(8,128)S(1)} %bitcast.29), kind=kOutput, calls=%fused_computation.25 | output fusion | flops 1835135 | bytes 7368704 | tf_op jit(solution)/shard_map/while/body/eval_jaxpr/sub | solution.py:42
  181.3 0.0 copy-start.1
  181.3 0.0 copy-start.3
  181.3 0.0 copy-start.2
  181.4 1.2 broadcast_divide_fusion
  182.6 0.1 broadcast_in_dim.30
  182.7 0.2 ge.15
  182.9 0.0 copy-done.1
  182.9 0.1 and_bitcast_fusion
  183.0 0.5 fusion.1
  183.5 30.6 %all-gather = f32[64,128]{1,0:T(8,128)S(1)} all-gather(f32[8,128]{1,0:T(8,128)S(1)} %bitcast.34), channel_id=2, replica_groups=mesh['seq'=8,'kvh'=4] {'seq'}, dimensions={0}, use_global_device_ids=true | all-gather | bytes 36864 | tf_op jit(solution)/shard_map/all_gather | solution.py:46
  214.1 0.3 fusion.13
  214.4 0.0 copy-done.3
  214.4 0.1 fusion.8
  214.5 0.0 copy-done.2
  214.5 0.3 fusion.4
  214.8 0.0 copy-start
  214.8 30.5 %all_gather.11 = bf16[512,128]{1,0:T(8,128)(2,1)S(1)} all-gather(bf16[64,128]{1,0:T(8,128)(2,1)S(1)} %fusion.4), channel_id=1, replica_groups=mesh['seq'=8,'kvh'=4] {'seq'}, dimensions={0}, use_global_device_ids=true | all-gather | bytes 147456 | tf_op jit(solution)/shard_map/all_gather | solution.py:63
  245.3 0.4 fusion.3
  245.7 0.5 copy.15
  246.3 0.3 reshape.33
  246.6 1.2 copy.16
  247.8 0.0 copy-done
  (6 shorter events, 0.0 us)
Async XLA Ops:
  181.3 1.6 copy-start.1
  181.3 33.1 %copy-start.3 = (s32[8]{0:T(128)S(1)}, s32[8]{0:T(128)}, u32[]{:S(2)}) copy-start(s32[8]{0:T(128)} %param.9) | copy-start | bytes 100
  181.3 33.2 %copy-start.2 = (bf16[64,1,128]{2,0,1:T(8,128)(2,1)S(1)}, bf16[64,1,128]{2,0,1:T(8,128)(2,1)}, u32[]{:S(2)}) copy-start(bf16[64,1,128]{2,0,1:T(8,128)(2,1)} %param.7) | copy-start | bytes 49156
  214.8 33.0 %copy-start = (bf16[64,128]{1,0:T(8,128)(2,1)}, bf16[64,128]{1,0:T(8,128)(2,1)S(1)}, u32[]{:S(2)}) copy-start(bf16[64,128]{1,0:T(8,128)(2,1)S(1)} %fusion.4) | copy-start | bytes 49156
